TPU v7x, 32 devices: a whole 2x2x4 slice. The times are simulated.
32 devices in a mesh: img: 8 (over z, core), txt: 4 (over y, x).
Axes of the slice: x: 2, y: 2, z: 4, core: 2. Of those that a mesh axis runs over, the one named last changes fastest.
Arguments:
- teacher_img: bfloat16 [8192, 1280], P('img'), may hold values from -40 to 40
- teacher_txt: bfloat16 [4096, 1280], P('txt'), may hold values from -40 to 40
- student_img: bfloat16 [8192, 512], P('img'), may hold values from -40 to 40
- student_txt: bfloat16 [4096, 512], P('txt'), may hold values from -40 to 40
Outputs:
- loss: float32 [], replicated
- grad_img: float32 [8192, 512], P(('img', 'txt'))
- grad_txt: float32 [4096, 512], P(('txt', 'img'))
All inputs are finite; a program needn't handle non-finite values.
Results may differ from a plain program's by a relative error of at most 0.0033.
Values sent between devices are 32-bit elements; how exact they have to be, the bound alone decides.
A program may use at most 64 MiB of HBM per device.

v0:
```python
import math

import jax
import jax.numpy as jnp
from jax import lax
from jax.sharding import PartitionSpec as P


def body(teacher_img, teacher_txt, student_img, student_txt):
    scale_teach = 3.0 / math.sqrt(teacher_img.shape[1])
    scale_learn = 3.0 / math.sqrt(student_img.shape[1])
    rows = teacher_img.shape[0]
    cols = teacher_txt.shape[0]
    img_count = lax.axis_size("img")
    txt_count = lax.axis_size("txt")
    teacher = scale_teach * jnp.einsum(
        "id,jd->ij", teacher_img, teacher_txt, preferred_element_type=jnp.float32
    )
    student = scale_learn * jnp.einsum(
        "id,jd->ij", student_img, student_txt, preferred_element_type=jnp.float32
    )
    row_tpeak, row_lpeak = lax.pmax((jnp.max(teacher, axis=1), jnp.max(student, axis=1)), "txt")
    col_tpeak, col_lpeak = lax.pmax((jnp.max(teacher, axis=0), jnp.max(student, axis=0)), "img")
    row_tmass, row_lmass = lax.psum(
        (
            jnp.sum(jnp.exp(teacher - row_tpeak[:, None]), axis=1),
            jnp.sum(jnp.exp(student - row_lpeak[:, None]), axis=1),
        ),
        "txt",
    )
    col_tmass, col_lmass = lax.psum(
        (
            jnp.sum(jnp.exp(teacher - col_tpeak[None, :]), axis=0),
            jnp.sum(jnp.exp(student - col_lpeak[None, :]), axis=0),
        ),
        "img",
    )
    row_teach = row_tpeak + jnp.log(row_tmass)
    row_learn = row_lpeak + jnp.log(row_lmass)
    col_teach = col_tpeak + jnp.log(col_tmass)
    col_learn = col_lpeak + jnp.log(col_lmass)
    p_row = jnp.exp(teacher - row_teach[:, None])
    q_row = jnp.exp(student - row_learn[:, None])
    p_col = jnp.exp(teacher - col_teach[None, :])
    q_col = jnp.exp(student - col_learn[None, :])
    gap = teacher - student
    row_part = (jnp.sum(p_row * gap) + jnp.sum(row_learn - row_teach) / txt_count) / (
        rows * img_count
    )
    col_part = (jnp.sum(p_col * gap) + jnp.sum(col_learn - col_teach) / img_count) / (
        cols * txt_count
    )
    delta = (8.0 * (q_row - p_row + q_col - p_col)).astype(jnp.bfloat16)
    loss = 0.5 * lax.psum(row_part + col_part, ("img", "txt"))
    picked = delta
    grad_txt = lax.psum_scatter(
        scale_learn
        * jnp.einsum("ij,id->jd", picked, student_img, preferred_element_type=jnp.float32),
        "img",
        scatter_dimension=0,
        tiled=True,
    )
    picked = delta
    grad_img = lax.psum_scatter(
        scale_learn * jnp.dot(picked, student_txt, preferred_element_type=jnp.float32),
        "txt",
        scatter_dimension=0,
        tiled=True,
    )
    return (loss, grad_img, grad_txt)


def solution(mesh):
    placed = (P("img", None), P("txt", None), P("img", None), P("txt", None))
    return jax.shard_map(
        body,
        mesh=mesh,
        in_specs=placed,
        out_specs=(P(), P(("img", "txt"), None), P(("txt", "img"), None)),
        check_vma=False,
    )
```

profile of v0, /device:TPU:0, one launch (start us, length us, event | category | flops | bytes accessed | tf_op | source)
XLA Modules:
  0.0 193.4 jit_solution(10971360036748988000)
XLA Ops:
  7.2 0.0 copy-start
  7.2 0.0 reduce-scatter.3.cloned.1.call-start
  7.2 1.7 copy-done
  8.9 0.0 copy-start.2
  8.9 0.0 copy-start.4
  8.9 6.4 %multiply_reduce_fusion.4 = (f32[1024]{0:T(1024)S(1)}, f32[1024]{0:T(1024)S(1)}, f32[1024,1024]{1,0:T(8,128)}) fusion(bf16[1024,1280]{1,0:T(8,128)(2,1)S(1)} %copy-done, bf16[1024,1280]{1,0:T(8,128)(2,1)} %param.5), kind=kOutput, calls=%fused_computation.12 | convolution fusion | flops 2687498240 | bytes 9445376 | tf_op jit(solution)/shard_map/id,jd->ij/dot_general | solution.py:16
  15.3 0.0 copy-done.2
  15.3 0.0 copy-done.4
  15.3 3.2 %multiply_reduce_fusion.2 = (f32[1024]{0:T(1024)S(1)}, f32[1024]{0:T(1024)S(1)}, f32[1024,1024]{1,0:T(8,128)}) fusion(bf16[1024,512]{1,0:T(8,128)(2,1)S(1)} %copy-done.4, bf16[1024,512]{1,0:T(8,128)(2,1)S(1)} %copy-done.2), kind=kOutput, calls=%fused_computation.9 | convolution fusion | flops 1076885504 | bytes 6299648 | tf_op jit(solution)/shard_map/id,jd->ij/dot_general | solution.py:19
  18.5 18.3 %all-reduce = (f32[1024]{0:T(1024)S(1)}, f32[1024]{0:T(1024)S(1)}) all-reduce(f32[1024]{0:T(1024)S(1)} %get-tuple-element.11, f32[1024]{0:T(1024)S(1)} %get-tuple-element.6), channel_id=1, replica_groups=mesh['img'=8,'txt'=4] {'img'}, use_global_device_ids=true, to_apply=%region_11.0 | all-reduce | flops 2048 | bytes 16384 | tf_op jit(solution)/shard_map/pmax | solution.py:23
  36.9 10.1 %all-reduce.1 = (f32[1024]{0:T(1024)S(1)}, f32[1024]{0:T(1024)S(1)}) all-reduce(f32[1024]{0:T(1024)S(1)} %get-tuple-element.12, f32[1024]{0:T(1024)S(1)} %get-tuple-element.7), channel_id=1, replica_groups=mesh['img'=8,'txt'=4] {'txt'}, use_global_device_ids=true, to_apply=%region_1.0 | all-reduce | flops 2048 | bytes 16384 | tf_op jit(solution)/shard_map/pmax | solution.py:22
  47.0 3.7 %exponential_reduce_fusion.1 = (f32[1024]{0:T(1024)S(1)}, f32[1024]{0:T(1024)S(1)}) fusion(f32[1024,1024]{1,0:T(8,128)} %get-tuple-element.21, f32[1024]{0:T(1024)S(1)} %get-tuple-element.13, f32[1024]{0:T(1024)S(1)} %get-tuple-element.15), kind=kLoop, calls=%fused_computation.4 | loop fusion | flops 5240832 | bytes 4210688 | tf_op jit(solution)/shard_map/reduce_sum | solution.py:33
  50.7 13.6 %psum.37 = f32[1024]{0:T(1024)S(1)} all-reduce(f32[1024]{0:T(1024)S(1)} %get-tuple-element.9), channel_id=1, replica_groups=mesh['img'=8,'txt'=4] {'img'}, use_global_device_ids=true, to_apply=%region_13.0 | all-reduce | flops 1024 | bytes 8192 | tf_op jit(solution)/shard_map/psum | solution.py:31
  64.3 7.9 %psum.35 = f32[1024]{0:T(1024)S(1)} all-reduce(f32[1024]{0:T(1024)S(1)} %get-tuple-element.10), channel_id=1, replica_groups=mesh['img'=8,'txt'=4] {'txt'}, use_global_device_ids=true, to_apply=%region_3.0 | all-reduce | flops 1024 | bytes 8192 | tf_op jit(solution)/shard_map/psum | solution.py:24
  72.2 8.1 %multiply_reduce_fusion = (f32[]{:T(128)}, f32[]{:T(128)}, f32[1024]{0:T(1024)S(1)}, f32[1024]{0:T(1024)S(1)}) fusion(f32[1024,1024]{1,0:T(8,128)} %get-tuple-element.22, f32[1024,1024]{1,0:T(8,128)} %get-tuple-element.21, f32[1024]{0:T(1024)S(1)} %log_add_fusion.1, f32[1024]{0:T(1024)S(1)} %log_add_fusion.3, f32[1024]{0:T(1024)S(1)} %get-tuple-element.14, ...), kind=kLoop, calls=%fused_computation.2 | loop fusion | flops 13629438 | bytes 8413192 | tf_op jit(solution)/shard_map/reduce_sum | solution.py:50
  80.4 13.6 %psum.38 = f32[1024]{0:T(1024)S(1)} all-reduce(f32[1024]{0:T(1024)S(1)} %get-tuple-element.5), channel_id=1, replica_groups=mesh['img'=8,'txt'=4] {'img'}, use_global_device_ids=true, to_apply=%region_18.0 | all-reduce | flops 1024 | bytes 8192 | tf_op jit(solution)/shard_map/psum | solution.py:31
  93.9 0.6 subtract_reduce_fusion
  94.5 9.0 %psum.36 = f32[1024]{0:T(1024)S(1)} all-reduce(f32[1024]{0:T(1024)S(1)} %get-tuple-element.8), channel_id=1, replica_groups=mesh['img'=8,'txt'=4] {'txt'}, use_global_device_ids=true, to_apply=%region_8.0 | all-reduce | flops 1024 | bytes 8192 | tf_op jit(solution)/shard_map/psum | solution.py:24
  103.5 0.6 subtract_reduce_fusion.1
  104.2 0.0 copy-start.3
  104.2 5.1 %multiply_convert_fusion = bf16[1024,1024]{1,0:T(8,128)(2,1)S(1)} fusion(f32[1024,1024]{1,0:T(8,128)} %get-tuple-element.22, f32[1024,1024]{1,0:T(8,128)} %get-tuple-element.21, f32[1024]{0:T(1024)S(1)} %get-tuple-element.18, f32[1024]{0:T(1024)S(1)} %get-tuple-element.20, f32[1024]{0:T(1024)S(1)} %log_add_fusion.1, f32[1024]{0:T(1024)S(1)} %log_add_fusion.3), kind=kLoop, calls=%fused_computation | loop fusion | flops 11534336 | bytes 10502144 | tf_op jit(solution)/shard_map/convert_element_type | solution.py:53
  109.2 0.0 copy-start.1
  109.2 1.3 copy-done.1
  110.6 0.0 copy-done.3
  110.6 2.6 %convolution_multiply_fusion.1 = f32[1024,512]{1,0:T(8,128)} fusion(bf16[1024,1024]{1,0:T(8,128)(2,1)S(1)} %multiply_convert_fusion, bf16[1024,512]{1,0:T(8,128)(2,1)S(1)} %copy-done.3), kind=kOutput, calls=%fused_computation.15 | convolution fusion | flops 1074266112 | bytes 5242880 | tf_op jit(solution)/shard_map/dot_general | solution.py:65
  113.2 0.0 reduce-scatter.3.cloned.1.call-update
  113.2 0.0 reduce-scatter.5.cloned.1.call-start
  113.2 4.4 %convolution_multiply_fusion = f32[1024,512]{1,0:T(8,128)} fusion(bf16[1024,1024]{1,0:T(8,128)(2,1)} %copy-done.1, bf16[1024,512]{1,0:T(8,128)(2,1)} %param.6), kind=kOutput, calls=%fused_computation.14 | convolution fusion | flops 1074266112 | bytes 5242880 | tf_op jit(solution)/shard_map/ij,id->jd/dot_general | solution.py:58
  117.7 0.0 reduce-scatter.5.cloned.1.call-update
  120.1 37.2 %psum.39 = f32[]{:T(128)} all-reduce(f32[]{:T(128)S(6)} %add.44), channel_id=1, replica_groups=mesh['img'=8,'txt'=4] {'img','txt'}, use_global_device_ids=true, to_apply=%region_20.0 | all-reduce | flops 1 | bytes 8 | tf_op jit(solution)/shard_map/psum | solution.py:54
  158.0 0.0 reduce-scatter.3.cloned.1.call-done
  158.0 27.5 %reduce-scatter.5.cloned.1.call-done = f32[128,512]{1,0:T(8,128)} async-done(((f32[1024,512]{1,0:T(8,128)}), f32[128,512]{1,0:T(8,128)}) %reduce-scatter.5.cloned.1.call-update) | async-done | bytes 262160 | tf_op jit(solution)/shard_map/reduce_scatter | solution.py:56
  (2 shorter events, 0.0 us)
Async XLA Ops:
  7.2 1.7 copy-start
  7.2 150.8 %reduce-scatter.3.cloned.1.call-start = ((), (), s32[]{:S(2)}) async-start(), calls=%async_computation.2 | async-start | bytes 2621440 | tf_op jit(solution)/shard_map/reduce_scatter | solution.py:64
  8.9 6.4 %copy-start.2 = (bf16[1024,512]{1,0:T(8,128)(2,1)S(1)}, bf16[1024,512]{1,0:T(8,128)(2,1)}, u32[]{:S(2)}) copy-start(bf16[1024,512]{1,0:T(8,128)(2,1)} %param.7) | copy-start | bytes 3145732
  8.9 6.4 %copy-start.4 = (bf16[1024,512]{1,0:T(8,128)(2,1)S(1)}, bf16[1024,512]{1,0:T(8,128)(2,1)}, u32[]{:S(2)}) copy-start(bf16[1024,512]{1,0:T(8,128)(2,1)} %param.6) | copy-start | bytes 3145732
  104.2 6.4 %copy-start.3 = (bf16[1024,512]{1,0:T(8,128)(2,1)S(1)}, bf16[1024,512]{1,0:T(8,128)(2,1)}, u32[]{:S(2)}) copy-start(bf16[1024,512]{1,0:T(8,128)(2,1)} %param.7) | copy-start | bytes 3145732
  109.2 1.3 copy-start.1
  113.2 72.3 %reduce-scatter.5.cloned.1.call-start = ((), (), s32[]{:S(2)}) async-start(), calls=%async_computation.3 | async-start | bytes 2359296 | tf_op jit(solution)/shard_map/reduce_scatter | solution.py:56
Sparse Core Ops, SparseCore 0:
  113.3 33.0 reduce-scatter.2
  149.3 36.1 reduce-scatter.4
where the time goes:
time: 194 us; the launch traced here: 193 us
  blocking collectives  110 us (57%)
  waiting for transfers between devices  27.5 us (14%)
  between operations  18.3 us (9%)
  other arithmetic  18.2 us (9%)
  matrix products  16.7 us (9%)
  local copies, waits for them, and re-layouts  3.03 us (2%)
    psum x1, blocking collectives, body(): loss = 0.5 * lax.psum(row_part + col_part, ('img', 'txt'))  37.2 us
    reduce_scatter x1, waiting for transfers between devices, body(): lax.psum_scatter(scale_learn * jnp.einsum('ij,id->jd', picked, student_im...  27.5 us
    psum x2, blocking collectives, body(): lax.psum((jnp.sum(jnp.exp(teacher - col_tpeak[None, :]), axis=0), jnp.sum...  27.2 us
    pmax x1, blocking collectives, body(): lax.pmax((jnp.max(teacher, axis=0), jnp.max(student, axis=0)), 'img')  18.3 us
    psum x2, blocking collectives, body(): lax.psum((jnp.sum(jnp.exp(teacher - row_tpeak[:, None]), axis=1), jnp.sum...  16.9 us
    pmax x1, blocking collectives, body(): lax.pmax((jnp.max(teacher, axis=1), jnp.max(student, axis=1)), 'txt')  10.1 us
    reduce_sum x1, other arithmetic, body(): jnp.sum(p_col * gap) + jnp.sum(col_learn - col_teach) / img_count  8.12 us
    dot_general x1, matrix products, body(): jnp.einsum('id,jd->ij', teacher_img, teacher_txt, preferred_element_type=...  6.41 us
  transfers between devices with their start and end apart: 2, of which 1 were waited for; matrix products, arithmetic and copies ran while one was open for 2% of the time, Pallas kernels for 0%

commit v1 on v0

v1 whole, which is shorter than its diff:
```python
import functools
import math

import jax
import jax.numpy as jnp
from jax import lax
from jax.experimental import pallas as pl
from jax.experimental.pallas import tpu as pltpu
from jax.sharding import PartitionSpec as P

LANES = 128
LOG2E = math.log2(math.e)
LN2 = math.log(2.0)
MESH = pl.DeviceIdType.MESH
F32 = jnp.float32
NT = (((1,), (1,)), ((), ()))


def kernel(
    img_n, txt_n,
    timg_hbm, ttxt_hbm, simg_hbm, stxt_hbm,
    loss_ref, gimg_ref, gtxt_ref,
    timg, ttxt, simg, stxt, t2, s2, rows_col, cstat, rslot, cslot, delta, deltat,
    gi, gir, gt, xr, gtr, lrow, lcol,
    in_sem, rs_send, rs_recv, cs_send, cs_recv, gi_send, gi_recv, x_send, x_recv,
    gt_send, gt_recv, l1_send, l1_recv, l2_send, l2_recv,
):
    rows, wide = timg.shape
    cols, deep = stxt.shape
    strips = rows // LANES
    pieces = cols // LANES
    mi = lax.axis_index("img")
    mt = lax.axis_index("txt")
    levels = img_n // 2
    mz = mi // 2
    mc = lax.rem(mi, 2)
    scale_t = 3.0 / math.sqrt(wide) * LOG2E
    scale_s = 3.0 / math.sqrt(deep) * LOG2E
    scale_g = 3.0 / math.sqrt(deep)

    loads = [
        pltpu.make_async_copy(src, dst, in_sem.at[k])
        for k, (src, dst) in enumerate(
            ((stxt_hbm, stxt), (simg_hbm, simg), (ttxt_hbm, ttxt), (timg_hbm, timg))
        )
    ]
    for load in loads:
        load.start()

    barrier = pltpu.get_barrier_semaphore()
    txt_peers = [lax.rem(mt + d, txt_n) for d in range(1, txt_n)]
    img_peers = [lax.rem(mi + d, img_n) for d in range(1, img_n)]
    for p in txt_peers:
        pl.semaphore_signal(barrier, inc=1, device_id=(mi, p), device_id_type=MESH)
    for p in img_peers:
        pl.semaphore_signal(barrier, inc=1, device_id=(p, mt), device_id_type=MESH)

    def to_txt(src, dst, send, recv, p):
        return pltpu.make_async_remote_copy(
            src_ref=src, dst_ref=dst, send_sem=send, recv_sem=recv,
            device_id=(mi, p), device_id_type=MESH,
        )

    def to_img(src, dst, send, recv, p):
        return pltpu.make_async_remote_copy(
            src_ref=src, dst_ref=dst, send_sem=send, recv_sem=recv,
            device_id=(p, mt), device_id_type=MESH,
        )

    lane = lax.broadcasted_iota(jnp.int32, (8, LANES), 1)

    loads[0].wait()
    loads[1].wait()

    def student_strip(k, c):
        at = pl.ds(pl.multiple_of(k * LANES, LANES), LANES)
        s2[at, :] = scale_s * lax.dot_general(
            simg[at, :], stxt[...], NT, preferred_element_type=F32
        )
        return c

    lax.fori_loop(0, strips, student_strip, 0)
    loads[2].wait()
    loads[3].wait()

    cstat[0:1, :] = jnp.full((1, cols), -jnp.inf, F32)
    cstat[1:2, :] = jnp.zeros((1, cols), F32)
    cstat[2:3, :] = jnp.full((1, cols), -jnp.inf, F32)
    cstat[3:4, :] = jnp.zeros((1, cols), F32)

    def teacher_strip(k, c):
        at = pl.ds(pl.multiple_of(k * LANES, LANES), LANES)
        tt = scale_t * lax.dot_general(
            timg[at, :], ttxt[...], NT, preferred_element_type=F32
        )
        t2[at, :] = tt
        peak_t = jnp.max(tt, axis=0, keepdims=True)
        peak_s = jnp.max(s2[at, :], axis=0, keepdims=True)

        def group(g, mass):
            mass_t, mass_s = mass
            here = pl.ds(pl.multiple_of(k * LANES + g * 8, 8), 8)
            tg = t2[here, :]
            sg = s2[here, :]
            rt = jnp.max(tg, axis=1, keepdims=True)
            rs = jnp.max(sg, axis=1, keepdims=True)
            st = jnp.sum(jnp.exp2(tg - rt), axis=1, keepdims=True)
            ss = jnp.sum(jnp.exp2(sg - rs), axis=1, keepdims=True)
            rows_col[here, :] = jnp.where(
                lane == 0, rt, jnp.where(lane == 1, st, jnp.where(lane == 2, rs, ss))
            )
            return (mass_t + jnp.exp2(tg - peak_t), mass_s + jnp.exp2(sg - peak_s))

        zero = jnp.zeros((8, cols), F32)
        mass_t, mass_s = lax.fori_loop(0, LANES // 8, group, (zero, zero), unroll=4)
        for q, (peak, mass) in enumerate(((peak_t, mass_t), (peak_s, mass_s))):
            old = cstat[2 * q : 2 * q + 1, :]
            top = jnp.maximum(old, peak)
            cstat[2 * q + 1 : 2 * q + 2, :] = cstat[2 * q + 1 : 2 * q + 2, :] * jnp.exp2(
                old - top
            ) + jnp.sum(mass, axis=0, keepdims=True) * jnp.exp2(peak - top)
            cstat[2 * q : 2 * q + 1, :] = top
        return c

    lax.fori_loop(0, strips, teacher_strip, 0)

    for k in range(pieces):
        part = cstat[:, k * LANES : (k + 1) * LANES]
        for q in range(4):
            cslot[mi, q, k : k + 1, :] = part[q : q + 1, :]
    for k in range(strips):
        turned = rows_col[k * LANES : (k + 1) * LANES, :].T
        for q in range(4):
            rslot[mt, q, k : k + 1, :] = turned[q : q + 1, :]

    pl.semaphore_wait(barrier, txt_n - 1 + img_n - 1)

    stat_out = []
    for d, p in enumerate(img_peers):
        stat_out.append(to_img(cslot.at[mi], cslot.at[mi], cs_send.at[d], cs_recv.at[mi], p))
    for d, p in enumerate(txt_peers):
        stat_out.append(to_txt(rslot.at[mt], rslot.at[mt], rs_send.at[d], rs_recv.at[mt], p))
    for copy in stat_out:
        copy.start()
    for d, p in enumerate(txt_peers):
        to_txt(rslot.at[p], rslot.at[p], rs_send.at[d], rs_recv.at[p], p).wait_recv()

    def joined(slot, n, q):
        peaks = [slot[k, 2 * q] for k in range(n)]
        top = functools.reduce(jnp.maximum, peaks)
        mass = functools.reduce(
            jnp.add, [slot[k, 2 * q + 1] * jnp.exp2(peaks[k] - top) for k in range(n)]
        )
        return top + jnp.log(mass) * LOG2E

    row_t = joined(rslot, txt_n, 0)
    row_s = joined(rslot, txt_n, 1)
    pad = jnp.zeros((LANES - 2, LANES), F32)
    for k in range(strips):
        rows_col[k * LANES : (k + 1) * LANES, :] = jnp.concatenate(
            [row_t[k : k + 1], row_s[k : k + 1], pad], axis=0
        ).T
    for d, p in enumerate(img_peers):
        to_img(cslot.at[p], cslot.at[p], cs_send.at[d], cs_recv.at[p], p).wait_recv()
    col_t = joined(cslot, img_n, 0)
    col_s = joined(cslot, img_n, 1)
    for k in range(pieces):
        cstat[0:1, k * LANES : (k + 1) * LANES] = col_t[k : k + 1]
        cstat[1:2, k * LANES : (k + 1) * LANES] = col_s[k : k + 1]

    def delta_strip(start):
        def group(g, c):
            here = pl.ds(pl.multiple_of(start + g * 16, 16), 16)
            ends = rows_col[here, :]
            tg = t2[here, :]
            sg = s2[here, :]
            d = (
                jnp.exp2(sg - ends[:, 1:2])
                - jnp.exp2(tg - ends[:, 0:1])
                + jnp.exp2(sg - cstat[1:2, :])
                - jnp.exp2(tg - cstat[0:1, :])
            )
            delta[here, :] = (8.0 * d).astype(jnp.bfloat16)
            return c

        lax.fori_loop(0, LANES // 16, group, 0, unroll=2)
        at = pl.ds(pl.multiple_of(start, LANES), LANES)
        deltat[:, at] = delta[at, :].T

    per = rows // txt_n
    cper = cols // img_n

    def rows_of(p):
        return pl.ds(pl.multiple_of(p * per, per), per)

    def cols_of(o):
        return pl.ds(pl.multiple_of(o * cper, cper), cper)

    fine = per % LANES == 0
    if not fine:
        lax.fori_loop(0, strips, lambda k, c: (delta_strip(k * LANES), c)[1], 0)

    gi_out = []
    for d, p in enumerate([*txt_peers, mt]):
        if fine:
            lax.fori_loop(
                0, per // LANES, lambda k, c, p=p: (delta_strip(p * per + k * LANES), c)[1], 0
            )
        gi[rows_of(p), :] = scale_g * jnp.dot(
            delta[rows_of(p), :], stxt[...], preferred_element_type=F32
        )
        if d < txt_n - 1:
            copy = to_txt(gi.at[rows_of(p), :], gir.at[mt], gi_send.at[d], gi_recv.at[mt], p)
            copy.start()
            gi_out.append(copy)

    def text_term(o):
        gt[cols_of(o), :] = scale_g * jnp.dot(
            deltat[cols_of(o), :], simg[...], preferred_element_type=F32
        )

    mate = mi + 1 - 2 * mc
    order = [lax.rem(mz + d, levels) for d in range(1, levels)]
    x_out = []
    for d, z in enumerate([*order, mz]):
        o = 2 * z + 1 - mc
        text_term(o)
        copy = to_img(gt.at[cols_of(o), :], xr.at[z], x_send.at[d], x_recv.at[z], mate)
        copy.start()
        x_out.append(copy)
    for z in [*order, mz]:
        text_term(2 * z + mc)
    gt_out = []
    for d, z in enumerate([*order, mz]):
        o = 2 * z + mc
        to_img(xr.at[z], xr.at[z], x_send.at[d], x_recv.at[z], mate).wait_recv()
        gt[cols_of(o), :] = gt[cols_of(o), :] + xr[z]
        if d < levels - 1:
            copy = to_img(gt.at[cols_of(o), :], gtr.at[mz], gt_send.at[d], gt_recv.at[mz], o)
            copy.start()
            gt_out.append(copy)

    def loss_group(g, acc):
        here = pl.ds(pl.multiple_of(g * 8, 8), 8)
        tg = t2[here, :]
        gap = tg - s2[here, :]
        p_row = jnp.exp2(tg - rows_col[here, 0:1])
        p_col = jnp.exp2(tg - cstat[0:1, :])
        both = (p_row * (1.0 / (rows * img_n)) + p_col * (1.0 / (cols * txt_n))) * gap
        return acc + both

    total = lax.fori_loop(0, rows // 8, loss_group, jnp.zeros((8, cols), F32), unroll=2)
    mine = (
        jnp.sum(total)
        + jnp.sum(row_s - row_t) * (1.0 / (rows * img_n * txt_n))
        + jnp.sum(col_s - col_t) * (1.0 / (cols * txt_n * img_n))
    )
    lrow[mt] = jnp.full((8, LANES), mine, F32)
    l1_out = [
        to_txt(lrow.at[mt], lrow.at[mt], l1_send.at[d], l1_recv.at[mt], p)
        for d, p in enumerate(txt_peers)
    ]
    for copy in l1_out:
        copy.start()
    for d, p in enumerate(txt_peers):
        to_txt(lrow.at[p], lrow.at[p], l1_send.at[d], l1_recv.at[p], p).wait_recv()
    lcol[mi] = functools.reduce(jnp.add, [lrow[k] for k in range(txt_n)])
    l2_out = [
        to_img(lcol.at[mi], lcol.at[mi], l2_send.at[d], l2_recv.at[mi], p)
        for d, p in enumerate(img_peers)
    ]
    for copy in l2_out:
        copy.start()
    for d, p in enumerate(img_peers):
        to_img(lcol.at[p], lcol.at[p], l2_send.at[d], l2_recv.at[p], p).wait_recv()
    loss_ref[...] = (0.5 * LN2) * functools.reduce(jnp.add, [lcol[k] for k in range(img_n)])

    for d, p in enumerate(txt_peers):
        to_txt(gir.at[p], gir.at[p], gi_send.at[d], gi_recv.at[p], p).wait_recv()
    gimg_ref[...] = functools.reduce(
        jnp.add, [gir[p] for p in txt_peers], gi[rows_of(mt), :]
    )
    for d, z in enumerate(order):
        to_img(gtr.at[z], gtr.at[z], gt_send.at[d], gt_recv.at[z], 2 * z + mc).wait_recv()
    gtxt_ref[...] = functools.reduce(
        jnp.add, [gtr[z] for z in order], gt[cols_of(mi), :]
    )
    for copy in [*stat_out, *gi_out, *x_out, *gt_out, *l1_out, *l2_out]:
        copy.wait_send()


def body(img_n, txt_n, teacher_img, teacher_txt, student_img, student_txt):
    rows, wide = teacher_img.shape
    cols, deep = student_txt.shape
    levels = img_n // 2
    vmem = pltpu.VMEM
    dma = pltpu.SemaphoreType.DMA
    bf16 = jnp.bfloat16
    loss, grad_img, grad_txt = pl.pallas_call(
        functools.partial(kernel, img_n, txt_n),
        out_shape=(
            jax.ShapeDtypeStruct((8, LANES), F32),
            jax.ShapeDtypeStruct((rows // txt_n, deep), F32),
            jax.ShapeDtypeStruct((cols // img_n, deep), F32),
        ),
        in_specs=[pl.BlockSpec(memory_space=pltpu.HBM)] * 4,
        out_specs=tuple(pl.BlockSpec(memory_space=vmem) for _ in range(3)),
        scratch_shapes=[
            vmem((rows, wide), bf16), vmem((cols, wide), bf16),
            vmem((rows, deep), bf16), vmem((cols, deep), bf16),
            vmem((rows, cols), F32), vmem((rows, cols), F32),
            vmem((rows, LANES), F32), vmem((8, cols), F32),
            vmem((txt_n, 4, rows // LANES, LANES), F32),
            vmem((img_n, 4, cols // LANES, LANES), F32),
            vmem((rows, cols), bf16), vmem((cols, rows), bf16),
            vmem((rows, deep), F32), vmem((txt_n, rows // txt_n, deep), F32),
            vmem((cols, deep), F32), vmem((levels, cols // img_n, deep), F32),
            vmem((levels, cols // img_n, deep), F32),
            vmem((txt_n, 8, LANES), F32), vmem((img_n, 8, LANES), F32),
            dma((4,)),
            dma((txt_n,)), dma((txt_n,)), dma((img_n,)), dma((img_n,)),
            dma((txt_n,)), dma((txt_n,)), dma((levels,)), dma((levels,)),
            dma((levels,)), dma((levels,)),
            dma((txt_n,)), dma((txt_n,)), dma((img_n,)), dma((img_n,)),
        ],
        compiler_params=pltpu.CompilerParams(
            collective_id=0, has_side_effects=True, vmem_limit_bytes=60 * 1024 * 1024
        ),
    )(teacher_img, teacher_txt, student_img, student_txt)
    return loss[0, 0], grad_img, grad_txt


def solution(mesh):
    placed = (P("img", None), P("txt", None), P("img", None), P("txt", None))
    return jax.shard_map(
        functools.partial(body, mesh.shape["img"], mesh.shape["txt"]),
        mesh=mesh,
        in_specs=placed,
        out_specs=(P(), P(("img", "txt"), None), P(("txt", "img"), None)),
        check_vma=False,
    )
```

time: 194 us -> 68.6 us (0.35)
  blocking collectives: 110 us -> 0 us
  Pallas kernels: 0 us -> 63 us
  waiting for transfers between devices: 27.5 us -> 0 us
  other arithmetic: 18.2 us -> 0 us
  between operations: 18.3 us -> 0.64 us
  matrix products: 16.7 us -> 0 us
    psum x5 -> x0, blocking collectives: 81.3 us -> none  [the longest x1 37.2 us: body(): loss = 0.5 * lax.psum(row_part + col_part, ('img', 'txt'))]
    pallas_call x0 -> x1, Pallas kernels: none -> 63 us  [body(): pl.pallas_call(functools.partial(kernel, img_n, txt_n), out_shape=(jax.Sh...]
    pmax x2 -> x0, blocking collectives: 28.4 us -> none  [the longest x1 18.3 us: body(): lax.pmax((jnp.max(teacher, axis=0), jnp.max(student, axis=0)), 'img')]
    reduce_scatter x2 -> x0, waiting for transfers between devices: 27.5 us -> none  [the longest x1 27.5 us: body(): lax.psum_scatter(scale_learn * jnp.einsum('ij,id->jd', picked, student_im...]
    dot_general x4 -> x0, matrix products: 16.7 us -> none  [the longest x1 6.41 us: body(): jnp.einsum('id,jd->ij', teacher_img, teacher_txt, preferred_element_type=...]
    reduce_sum x4 -> x0, other arithmetic: 13.1 us -> none  [the longest x1 8.12 us: body(): jnp.sum(p_col * gap) + jnp.sum(col_learn - col_teach) / img_count]
    convert_element_type x1 -> x0, other arithmetic: 5.05 us -> none  [body(): delta = (8.0 * (q_row - p_row + q_col - p_col)).astype(jnp.bfloat16)]
  transfers between devices with their start and end apart: 2 -> 0, of which waited for: 1 -> 0; matrix products, arithmetic and copies ran while one was open for 2% -> 0% of each run, Pallas kernels for 0% -> 0%
where the time goes in v1:
time: 68.6 us; the launch traced here: 68.4 us
  Pallas kernels  63 us (92%)
  local copies, waits for them, and re-layouts  4.72 us (7%)
    pallas_call x1, Pallas kernels, body(): pl.pallas_call(functools.partial(kernel, img_n, txt_n), out_shape=(jax.Sh...  63 us
    unnamed x2, local copies, waits for them, and re-layouts  3.54 us

profile of v1, /device:TPU:0, one launch (start us, length us, event | category | flops | bytes accessed | tf_op | source)
XLA Modules:
  0.0 68.4 jit_solution(2256632006941377276)
XLA Ops:
  0.6 63.0 %shard_map.67 = (f32[8,128]{1,0:T(8,128)}, f32[256,512]{1,0:T(8,128)}, f32[128,512]{1,0:T(8,128)}) custom-call(bf16[1024,1280]{1,0:T(8,128)(2,1)} %timg_hbm.1, bf16[1024,1280]{1,0:T(8,128)(2,1)} %ttxt_hbm.1, bf16[1024,512]{1,0:T(8,128)(2,1)} %simg_hbm.1, bf16[1024,512]{1,0:T(8,128)(2,1)} %stxt_hbm.1), custom_call_target="tpu_custom_call" | custom-call | tf_op jit(solution)/shard_map/pallas_call | solution.py:299
  63.7 1.2 %slice.3 = f32[1,1]{1,0:T(1,128)} slice(f32[8,128]{1,0:T(8,128)} %get-tuple-element.6), slice={[0:1], [0:1]} | slice | bytes 8 | tf_op jit(solution)/shard_map/slice | solution.py:330
  64.9 1.9 %copy.9 = f32[256,512]{1,0:T(8,128)} copy(f32[256,512]{1,0:T(8,128)} %get-tuple-element.13) | data formatting | bytes 1048576
  66.7 1.7 %copy.10 = f32[128,512]{1,0:T(8,128)} copy(f32[128,512]{1,0:T(8,128)} %get-tuple-element.14) | data formatting | bytes 524288

commit v2 on v1

v2 whole, which is shorter than its diff:
```python
import functools
import math

import jax
import jax.numpy as jnp
from jax import lax
from jax.experimental import pallas as pl
from jax.experimental.pallas import tpu as pltpu
from jax.sharding import PartitionSpec as P

LANES = 128
LOG2E = math.log2(math.e)
LN2 = math.log(2.0)
MESH = pl.DeviceIdType.MESH
F32 = jnp.float32
NT = (((1,), (1,)), ((), ()))


def kernel(
    img_n, txt_n,
    timg_hbm, ttxt_hbm, simg_hbm, stxt_hbm,
    loss_ref, gimg_ref, gtxt_ref,
    timg, ttxt, simg, stxt, t2, s2, row_at, cstat, rslot, cslot, delta, deltat,
    gi, gir, gt, xr, rr, rl, lrow, lcol,
    in_sem, rs_send, rs_recv, cs_send, cs_recv, gi_send, gi_recv, x_send, x_recv,
    z_send, z_recv, l1_send, l1_recv, l2_send, l2_recv,
):
    rows, wide = timg.shape
    cols, deep = stxt.shape
    strips = rows // LANES
    pieces = cols // LANES
    mi = lax.axis_index("img")
    mt = lax.axis_index("txt")
    levels = img_n // 2
    mz = mi // 2
    mc = lax.rem(mi, 2)
    scale_t = 3.0 / math.sqrt(wide) * LOG2E
    scale_s = 3.0 / math.sqrt(deep) * LOG2E
    scale_g = 3.0 / math.sqrt(deep)

    loads = [
        pltpu.make_async_copy(src, dst, in_sem.at[k])
        for k, (src, dst) in enumerate(
            ((timg_hbm, timg), (ttxt_hbm, ttxt), (simg_hbm, simg), (stxt_hbm, stxt))
        )
    ]
    for load in loads:
        load.start()

    barrier = pltpu.get_barrier_semaphore()
    txt_peers = [lax.rem(mt + d, txt_n) for d in range(1, txt_n)]
    img_peers = [lax.rem(mi + d, img_n) for d in range(1, img_n)]
    for p in txt_peers:
        pl.semaphore_signal(barrier, inc=1, device_id=(mi, p), device_id_type=MESH)
    for p in img_peers:
        pl.semaphore_signal(barrier, inc=1, device_id=(p, mt), device_id_type=MESH)

    def to_txt(src, dst, send, recv, p):
        return pltpu.make_async_remote_copy(
            src_ref=src, dst_ref=dst, send_sem=send, recv_sem=recv,
            device_id=(mi, p), device_id_type=MESH,
        )

    def to_img(src, dst, send, recv, p):
        return pltpu.make_async_remote_copy(
            src_ref=src, dst_ref=dst, send_sem=send, recv_sem=recv,
            device_id=(p, mt), device_id_type=MESH,
        )

    lane = lax.broadcasted_iota(jnp.int32, (8, LANES), 1)

    chunk = min(2 * LANES, cols)
    stat_out = []

    def product(left, right, out, factor, slot):
        def one(j, c):
            at = pl.ds(pl.multiple_of(j * chunk, chunk), chunk)
            tile = factor * lax.dot_general(
                left[...], right[at, :], NT, preferred_element_type=F32
            )
            out[:, at] = tile
            cstat[slot, 0:1, at] = jnp.max(tile, axis=0, keepdims=True)
            return c

        lax.fori_loop(0, cols // chunk, one, 0)

    def masses(out, slot):
        def group(g, mass):
            here = pl.ds(pl.multiple_of(g * 8, 8), 8)
            x = out[here, :]
            peak = jnp.max(x, axis=1, keepdims=True)
            row = jnp.sum(jnp.exp2(x - peak), axis=1, keepdims=True)
            row_at[slot, here, :] = jnp.where(lane == 0, peak, row)
            return mass + jnp.exp2(x - cstat[slot, 0:1, :])

        mass = lax.fori_loop(0, rows // 8, group, jnp.zeros((8, cols), F32), unroll=8)
        tops = cstat[slot, 0:1, :]
        sums = jnp.sum(mass, axis=0, keepdims=True)
        for k in range(pieces):
            at = slice(k * LANES, (k + 1) * LANES)
            cslot[slot, mi, 0, k : k + 1, :] = tops[:, at]
            cslot[slot, mi, 1, k : k + 1, :] = sums[:, at]
        for k in range(strips):
            turned = row_at[slot, k * LANES : (k + 1) * LANES, :].T
            rslot[slot, mt, 0, k : k + 1, :] = turned[0:1, :]
            rslot[slot, mt, 1, k : k + 1, :] = turned[1:2, :]
        if slot == 0:
            pl.semaphore_wait(barrier, txt_n - 1 + img_n - 1)
        copies = [
            to_img(
                cslot.at[slot, mi], cslot.at[slot, mi],
                cs_send.at[slot, d], cs_recv.at[slot, mi], p,
            )
            for d, p in reversed(list(enumerate(img_peers)))
        ] + [
            to_txt(
                rslot.at[slot, mt], rslot.at[slot, mt],
                rs_send.at[slot, d], rs_recv.at[slot, mt], p,
            )
            for d, p in enumerate(txt_peers)
        ]
        for copy in copies:
            copy.start()
        stat_out.extend(copies)

    loads[0].wait()
    loads[1].wait()
    product(timg, ttxt, t2, scale_t, 0)
    masses(t2, 0)
    loads[2].wait()
    loads[3].wait()
    product(simg, stxt, s2, scale_s, 1)
    masses(s2, 1)

    def joined(slot, n):
        peaks = [slot[k, 0] for k in range(n)]
        top = functools.reduce(jnp.maximum, peaks)
        mass = functools.reduce(
            jnp.add, [slot[k, 1] * jnp.exp2(peaks[k] - top) for k in range(n)]
        )
        return top + jnp.log(mass) * LOG2E

    pad = jnp.zeros((LANES - 8, LANES), F32)

    def gathered(slot):
        for d, p in enumerate(txt_peers):
            to_txt(
                rslot.at[slot, p], rslot.at[slot, p],
                rs_send.at[slot, d], rs_recv.at[slot, p], p,
            ).wait_recv()
        row = joined(rslot.at[slot], txt_n)
        for k in range(strips):
            row_at[slot, k * LANES : (k + 1) * LANES, :] = jnp.concatenate(
                [jnp.broadcast_to(row[k : k + 1], (8, LANES)), pad], axis=0
            ).T
        for d, p in enumerate(img_peers):
            to_img(
                cslot.at[slot, p], cslot.at[slot, p],
                cs_send.at[slot, d], cs_recv.at[slot, p], p,
            ).wait_recv()
        col = joined(cslot.at[slot], img_n)
        for k in range(pieces):
            cstat[slot, 0:1, k * LANES : (k + 1) * LANES] = col[k : k + 1]
        return row, col

    row_t, col_t = gathered(0)

    def teacher_group(g, acc):
        here = pl.ds(pl.multiple_of(g * 8, 8), 8)
        tg = t2[here, :]
        gap = tg - s2[here, :]
        p_row = jnp.exp2(tg - row_at[0, here, 0:1])
        p_col = jnp.exp2(tg - cstat[0, 0:1, :])
        t2[here, :] = p_row + p_col
        return acc + (
            p_row * (1.0 / (rows * img_n)) + p_col * (1.0 / (cols * txt_n))
        ) * gap

    total = lax.fori_loop(0, rows // 8, teacher_group, jnp.zeros((8, cols), F32), unroll=4)
    row_s, col_s = gathered(1)

    def delta_strip(start):
        def group(g, c):
            here = pl.ds(pl.multiple_of(start + g * 16, 16), 16)
            sg = s2[here, :]
            d = (
                jnp.exp2(sg - row_at[1, here, 0:1])
                + jnp.exp2(sg - cstat[1, 0:1, :])
                - t2[here, :]
            )
            delta[here, :] = (8.0 * d).astype(jnp.bfloat16)
            return c

        lax.fori_loop(0, LANES // 16, group, 0, unroll=4)
        at = pl.ds(pl.multiple_of(start, LANES), LANES)
        deltat[:, at] = delta[at, :].T

    per = rows // txt_n
    cper = cols // img_n

    def rows_of(p):
        return pl.ds(pl.multiple_of(p * per, per), per)

    def cols_of(o):
        return pl.ds(pl.multiple_of(o * cper, cper), cper)

    fine = per % LANES == 0
    if not fine:
        lax.fori_loop(0, strips, lambda k, c: (delta_strip(k * LANES), c)[1], 0)

    gi_out = []
    for d, p in enumerate([*txt_peers, mt]):
        if fine:
            lax.fori_loop(
                0, per // LANES, lambda k, c, p=p: (delta_strip(p * per + k * LANES), c)[1], 0
            )
        gi[rows_of(p), :] = scale_g * jnp.dot(
            delta[rows_of(p), :], stxt[...], preferred_element_type=F32
        )
        if d < txt_n - 1:
            copy = to_txt(gi.at[rows_of(p), :], gir.at[mt], gi_send.at[d], gi_recv.at[mt], p)
            copy.start()
            gi_out.append(copy)

    def text_term(o):
        gt[cols_of(o), :] = scale_g * jnp.dot(
            deltat[cols_of(o), :], simg[...], preferred_element_type=F32
        )

    mate = mi + 1 - 2 * mc
    high = (2 * mz) // levels
    ends_in = [k // 2 if k % 2 else levels - 1 - k // 2 for k in range(levels)]
    order = [e + high * (levels - 1 - 2 * e) for e in ends_in]
    x_out = []
    for d, b in enumerate(order):
        o = 2 * b + 1 - mc
        text_term(o)
        copy = to_img(gt.at[cols_of(o), :], xr.at[b], x_send.at[b], x_recv.at[b], mate)
        copy.start()
        x_out.append(copy)
    half = cper // 2

    def hop(b, h, way):
        slot = (rl, rr)[way].at[b, pl.ds(h * half, half), :]
        at = pl.ds(pl.multiple_of((2 * b + mc) * cper + h * half, half), half)
        return at, slot, to_img(
            gt.at[at, :], slot, z_send.at[way, b, h], z_recv.at[way, b, h],
            mi + (2 if way else -2),
        )

    def onward(b, h, way):
        at, slot, copy = hop(b, h, way)

        @pl.when(mz > 0 if way else mz < levels - 1)
        def _():
            copy.wait_recv()
            gt[at, :] = gt[at, :] + slot[...]

        copy.start()

    for d, b in enumerate(order):
        text_term(2 * b + mc)
        to_img(xr.at[b], xr.at[b], x_send.at[b], x_recv.at[b], mate).wait_recv()
        gt[cols_of(2 * b + mc), :] = gt[cols_of(2 * b + mc), :] + xr[b]

        @pl.when(b > mz)
        def _(b=b):
            onward(b, 0, 1)
            onward(b, 1, 1)

        @pl.when(b < mz)
        def _(b=b):
            onward(b, 0, 0)
            onward(b, 1, 0)

    mine = (
        jnp.sum(total)
        + jnp.sum(row_s - row_t) * (1.0 / (rows * img_n * txt_n))
        + jnp.sum(col_s - col_t) * (1.0 / (cols * txt_n * img_n))
    )
    lrow[mt] = jnp.full((8, LANES), mine, F32)
    l1_out = [
        to_txt(lrow.at[mt], lrow.at[mt], l1_send.at[d], l1_recv.at[mt], p)
        for d, p in enumerate(txt_peers)
    ]
    for copy in l1_out:
        copy.start()
    for d, p in enumerate(txt_peers):
        to_txt(lrow.at[p], lrow.at[p], l1_send.at[d], l1_recv.at[p], p).wait_recv()
    lcol[mi] = functools.reduce(jnp.add, [lrow[k] for k in range(txt_n)])
    l2_out = [
        to_img(lcol.at[mi], lcol.at[mi], l2_send.at[d], l2_recv.at[mi], p)
        for d, p in enumerate(img_peers)
    ]
    for copy in l2_out:
        copy.start()
    for d, p in enumerate(img_peers):
        to_img(lcol.at[p], lcol.at[p], l2_send.at[d], l2_recv.at[p], p).wait_recv()
    loss_ref[...] = (0.5 * LN2) * functools.reduce(jnp.add, [lcol[k] for k in range(img_n)])

    for d, p in enumerate(txt_peers):
        to_txt(gir.at[p], gir.at[p], gi_send.at[d], gi_recv.at[p], p).wait_recv()
    gimg_ref[...] = functools.reduce(
        jnp.add, [gir[p] for p in txt_peers], gi[rows_of(mt), :]
    )
    for way in (0, 1):
        @pl.when(mz > 0 if way else mz < levels - 1)
        def _(way=way):
            for h in range(2):
                at, slot, copy = hop(mz, h, way)
                copy.wait_recv()
                gt[at, :] = gt[at, :] + slot[...]

    gtxt_ref[...] = gt[cols_of(mi), :]
    for b in order:
        @pl.when(b > mz)
        def _(b=b):
            for h in range(2):
                hop(b, h, 1)[2].wait_send()

        @pl.when(b < mz)
        def _(b=b):
            for h in range(2):
                hop(b, h, 0)[2].wait_send()

    for copy in [*stat_out, *gi_out, *x_out, *l1_out, *l2_out]:
        copy.wait_send()


def hand_over(loss, gimg, gtxt, loss_out, gimg_out, gtxt_out):
    loss_out[0, 0] = loss[0, 0]
    gimg_out[...] = gimg[...]
    gtxt_out[...] = gtxt[...]


def body(img_n, txt_n, teacher_img, teacher_txt, student_img, student_txt):
    rows, wide = teacher_img.shape
    cols, deep = student_txt.shape
    levels = img_n // 2
    vmem = pltpu.VMEM
    dma = pltpu.SemaphoreType.DMA
    bf16 = jnp.bfloat16
    loss, grad_img, grad_txt = pl.pallas_call(
        functools.partial(kernel, img_n, txt_n),
        out_shape=(
            jax.ShapeDtypeStruct((8, LANES), F32),
            jax.ShapeDtypeStruct((rows // txt_n, deep), F32),
            jax.ShapeDtypeStruct((cols // img_n, deep), F32),
        ),
        in_specs=[pl.BlockSpec(memory_space=pltpu.HBM)] * 4,
        out_specs=tuple(pl.BlockSpec(memory_space=vmem) for _ in range(3)),
        scratch_shapes=[
            vmem((rows, wide), bf16), vmem((cols, wide), bf16),
            vmem((rows, deep), bf16), vmem((cols, deep), bf16),
            vmem((rows, cols), F32), vmem((rows, cols), F32),
            vmem((2, rows, LANES), F32), vmem((2, 8, cols), F32),
            vmem((2, txt_n, 2, rows // LANES, LANES), F32),
            vmem((2, img_n, 2, cols // LANES, LANES), F32),
            vmem((rows, cols), bf16), vmem((cols, rows), bf16),
            vmem((rows, deep), F32), vmem((txt_n, rows // txt_n, deep), F32),
            vmem((cols, deep), F32), vmem((levels, cols // img_n, deep), F32),
            vmem((levels, cols // img_n, deep), F32), vmem((levels, cols // img_n, deep), F32),
            vmem((txt_n, 8, LANES), F32), vmem((img_n, 8, LANES), F32),
            dma((4,)),
            dma((2, txt_n)), dma((2, txt_n)), dma((2, img_n)), dma((2, img_n)),
            dma((txt_n,)), dma((txt_n,)), dma((levels,)), dma((levels,)),
            dma((2, levels, 2)), dma((2, levels, 2)),
            dma((txt_n,)), dma((txt_n,)), dma((img_n,)), dma((img_n,)),
        ],
        compiler_params=pltpu.CompilerParams(
            collective_id=0, has_side_effects=True, vmem_limit_bytes=60 * 1024 * 1024
        ),
    )(teacher_img, teacher_txt, student_img, student_txt)
    loss, grad_img, grad_txt = pl.pallas_call(
        hand_over,
        out_shape=(
            jax.ShapeDtypeStruct((1, 1), F32),
            jax.ShapeDtypeStruct(grad_img.shape, F32),
            jax.ShapeDtypeStruct(grad_txt.shape, F32),
        ),
        in_specs=[pl.BlockSpec(memory_space=vmem)] * 3,
        out_specs=(
            pl.BlockSpec(memory_space=pltpu.SMEM),
            pl.BlockSpec(memory_space=vmem), pl.BlockSpec(memory_space=vmem),
        ),
    )(loss, grad_img, grad_txt)
    return loss.reshape(()), grad_img, grad_txt


def solution(mesh):
    placed = (P("img", None), P("txt", None), P("img", None), P("txt", None))
    return jax.shard_map(
        functools.partial(body, mesh.shape["img"], mesh.shape["txt"]),
        mesh=mesh,
        in_specs=placed,
        out_specs=(P(), P(("img", "txt"), None), P(("txt", "img"), None)),
        check_vma=False,
    )
```

time: 68.6 us -> 58.7 us (0.86)
  Pallas kernels: 63 us -> 57.9 us
  local copies, waits for them, and re-layouts: 4.72 us -> 0 us
    pallas_call x1, Pallas kernels: 63 us -> 55.8 us  [body(): pl.pallas_call(functools.partial(kernel, img_n, txt_n), out_shape=(jax.Sh...]
    unnamed x2 -> x0, local copies, waits for them, and re-layouts: 3.54 us -> none
    pallas_call x0 -> x1, Pallas kernels: none -> 2.03 us  [body(): pl.pallas_call(hand_over, out_shape=(jax.ShapeDtypeStruct((1, 1), F32), j...]
    slice x1 -> x0, local copies, waits for them, and re-layouts: 1.19 us -> none  [body(): return (loss[0, 0], grad_img, grad_txt)]
where the time goes in v2:
time: 58.7 us; the launch traced here: 58.5 us
  Pallas kernels  57.9 us (99%)
  between operations  0.64 us (1%)
    pallas_call x1, Pallas kernels, body(): pl.pallas_call(functools.partial(kernel, img_n, txt_n), out_shape=(jax.Sh...  55.8 us
    pallas_call x1, Pallas kernels, body(): pl.pallas_call(hand_over, out_shape=(jax.ShapeDtypeStruct((1, 1), F32), j...  2.03 us

profile of v2, /device:TPU:0, one launch (start us, length us, event | category | flops | bytes accessed | tf_op | source)
XLA Modules:
  0.0 58.5 jit_solution(14623818371618584722)
XLA Ops:
  0.6 55.8 %shard_map.67 = (f32[8,128]{1,0:T(8,128)}, f32[256,512]{1,0:T(8,128)}, f32[128,512]{1,0:T(8,128)}) custom-call(bf16[1024,1280]{1,0:T(8,128)(2,1)} %timg_hbm.1, bf16[1024,1280]{1,0:T(8,128)(2,1)} %ttxt_hbm.1, bf16[1024,512]{1,0:T(8,128)(2,1)} %simg_hbm.1, bf16[1024,512]{1,0:T(8,128)(2,1)} %stxt_hbm.1), custom_call_target="tpu_custom_call" | custom-call | tf_op jit(solution)/shard_map/pallas_call | solution.py:343
  56.5 2.0 %shard_map.68 = (f32[1,1]{1,0:T(1,128)}, f32[256,512]{1,0:T(8,128)}, f32[128,512]{1,0:T(8,128)}) custom-call(f32[8,128]{1,0:T(8,128)} %get-tuple-element.9.loss, f32[256,512]{1,0:T(8,128)} %get-tuple-element.10.gimg, f32[128,512]{1,0:T(8,128)} %get-tuple-element.11.gtxt), custom_call_target="tpu_custom_call" | custom-call | tf_op jit(solution)/shard_map/pallas_call | solution.py:374

commit v3 on v2

--- a/solution.py
+++ b/solution.py
@@ -16,13 +16,18 @@
 NT = (((1,), (1,)), ((), ()))
 
 
+def minor_of(n):
+    return 1 << ((n.bit_length() - 1) // 2)
+
+
 def kernel(
     img_n, txt_n,
     timg_hbm, ttxt_hbm, simg_hbm, stxt_hbm,
     loss_ref, gimg_ref, gtxt_ref,
     timg, ttxt, simg, stxt, t2, s2, row_at, cstat, rslot, cslot, delta, deltat,
-    gi, gir, gt, xr, rr, rl, lrow, lcol,
-    in_sem, rs_send, rs_recv, cs_send, cs_recv, gi_send, gi_recv, x_send, x_recv,
+    gi, g1a, g1b, g2a, g2b, gt, xr, rr, rl, lrow, lcol,
+    in_sem, rs_send, rs_recv, cs_send, cs_recv, a1_send, a1_recv, b1_send, b1_recv,
+    a2_send, a2_recv, b2_send, b2_recv, x_send, x_recv,
     z_send, z_recv, l1_send, l1_recv, l2_send, l2_recv,
 ):
     rows, wide = timg.shape
@@ -209,16 +214,73 @@
         lax.fori_loop(0, strips, lambda k, c: (delta_strip(k * LANES), c)[1], 0)
 
     gi_out = []
-    for d, p in enumerate([*txt_peers, mt]):
-        if fine:
-            lax.fori_loop(
-                0, per // LANES, lambda k, c, p=p: (delta_strip(p * per + k * LANES), c)[1], 0
-            )
-        gi[rows_of(p), :] = scale_g * jnp.dot(
-            delta[rows_of(p), :], stxt[...], preferred_element_type=F32
-        )
-        if d < txt_n - 1:
-            copy = to_txt(gi.at[rows_of(p), :], gir.at[mt], gi_send.at[d], gi_recv.at[mt], p)
+    minor = minor_of(txt_n)
+    major = txt_n // minor
+    my, mx = mt // minor, lax.rem(mt, minor)
+    part = per // 2
+
+    def block(y, x, w):
+        return pl.ds(pl.multiple_of((y * minor + x) * per + w * part, part), part)
+
+    ys = [lax.rem(my + d, major) for d in range(1, major)]
+    xs = [lax.rem(mx + d, minor) for d in range(1, minor)]
+    for y in [*ys, my]:
+        for x in [*xs, mx]:
+            p = y * minor + x
+            if fine:
+                lax.fori_loop(
+                    0, per // LANES,
+                    lambda k, c, p=p: (delta_strip(p * per + k * LANES), c)[1], 0,
+                )
+            gi[rows_of(p), :] = scale_g * jnp.dot(
+                delta[rows_of(p), :], stxt[...], preferred_element_type=F32
+            )
+            copies = []
+            if x is not mx:
+                copies.append(to_txt(
+                    gi.at[block(y, x, 0), :], g1a.at[mx, y],
+                    a1_send.at[x, y], a1_recv.at[mx, y], my * minor + x,
+                ))
+            if y is not my:
+                copies.append(to_txt(
+                    gi.at[block(y, x, 1), :], g1b.at[my, x],
+                    b1_send.at[y, x], b1_recv.at[my, x], y * minor + mx,
+                ))
+            for copy in copies:
+                copy.start()
+            gi_out.extend(copies)
+
+    def take_a(y):
+        for x in xs:
+            to_txt(
+                g1a.at[x, y], g1a.at[x, y], a1_send.at[x, y], a1_recv.at[x, y],
+                my * minor + x,
+            ).wait_recv()
+            gi[block(y, mx, 0), :] = gi[block(y, mx, 0), :] + g1a[x, y]
+
+    def take_b(x):
+        for y in ys:
+            to_txt(
+                g1b.at[y, x], g1b.at[y, x], b1_send.at[y, x], b1_recv.at[y, x],
+                y * minor + mx,
+            ).wait_recv()
+            gi[block(my, x, 1), :] = gi[block(my, x, 1), :] + g1b[y, x]
+
+    def second_leg():
+        for y in ys:
+            take_a(y)
+            copy = to_txt(
+                gi.at[block(y, mx, 0), :], g2a.at[my], a2_send.at[y], a2_recv.at[my],
+                y * minor + mx,
+            )
+            copy.start()
+            gi_out.append(copy)
+        for x in xs:
+            take_b(x)
+            copy = to_txt(
+                gi.at[block(my, x, 1), :], g2b.at[mx], b2_send.at[x], b2_recv.at[mx],
+                my * minor + x,
+            )
             copy.start()
             gi_out.append(copy)
 
@@ -259,6 +321,8 @@
         copy.start()
 
     for d, b in enumerate(order):
+        if d == levels // 2:
+            second_leg()
         text_term(2 * b + mc)
         to_img(xr.at[b], xr.at[b], x_send.at[b], x_recv.at[b], mate).wait_recv()
         gt[cols_of(2 * b + mc), :] = gt[cols_of(2 * b + mc), :] + xr[b]
@@ -298,11 +362,19 @@
         to_img(lcol.at[p], lcol.at[p], l2_send.at[d], l2_recv.at[p], p).wait_recv()
     loss_ref[...] = (0.5 * LN2) * functools.reduce(jnp.add, [lcol[k] for k in range(img_n)])
 
-    for d, p in enumerate(txt_peers):
-        to_txt(gir.at[p], gir.at[p], gi_send.at[d], gi_recv.at[p], p).wait_recv()
-    gimg_ref[...] = functools.reduce(
-        jnp.add, [gir[p] for p in txt_peers], gi[rows_of(mt), :]
-    )
+    take_a(my)
+    take_b(mx)
+    for y in ys:
+        to_txt(
+            g2a.at[y], g2a.at[y], a2_send.at[y], a2_recv.at[y], y * minor + mx
+        ).wait_recv()
+        gi[block(my, mx, 0), :] = gi[block(my, mx, 0), :] + g2a[y]
+    for x in xs:
+        to_txt(
+            g2b.at[x], g2b.at[x], b2_send.at[x], b2_recv.at[x], my * minor + x
+        ).wait_recv()
+        gi[block(my, mx, 1), :] = gi[block(my, mx, 1), :] + g2b[x]
+    gimg_ref[...] = gi[rows_of(mt), :]
     for way in (0, 1):
         @pl.when(mz > 0 if way else mz < levels - 1)
         def _(way=way):
@@ -338,6 +410,9 @@
     cols, deep = student_txt.shape
     levels = img_n // 2
     vmem = pltpu.VMEM
+    minor = minor_of(txt_n)
+    major = txt_n // minor
+    part = rows // txt_n // 2
     dma = pltpu.SemaphoreType.DMA
     bf16 = jnp.bfloat16
     loss, grad_img, grad_txt = pl.pallas_call(
@@ -357,13 +432,16 @@
             vmem((2, txt_n, 2, rows // LANES, LANES), F32),
             vmem((2, img_n, 2, cols // LANES, LANES), F32),
             vmem((rows, cols), bf16), vmem((cols, rows), bf16),
-            vmem((rows, deep), F32), vmem((txt_n, rows // txt_n, deep), F32),
+            vmem((rows, deep), F32), vmem((minor, major, part, deep), F32),
+            vmem((major, minor, part, deep), F32),
+            vmem((major, part, deep), F32), vmem((minor, part, deep), F32),
             vmem((cols, deep), F32), vmem((levels, cols // img_n, deep), F32),
             vmem((levels, cols // img_n, deep), F32), vmem((levels, cols // img_n, deep), F32),
             vmem((txt_n, 8, LANES), F32), vmem((img_n, 8, LANES), F32),
             dma((4,)),
             dma((2, txt_n)), dma((2, txt_n)), dma((2, img_n)), dma((2, img_n)),
-            dma((txt_n,)), dma((txt_n,)), dma((levels,)), dma((levels,)),
+            dma((minor, major)), dma((minor, major)), dma((major, minor)), dma((major, minor)),
+            dma((major,)), dma((major,)), dma((minor,)), dma((minor,)), dma((levels,)), dma((levels,)),
             dma((2, levels, 2)), dma((2, levels, 2)),
             dma((txt_n,)), dma((txt_n,)), dma((img_n,)), dma((img_n,)),
         ],

time: 58.7 us -> 57.1 us (0.973)
  Pallas kernels: 57.9 us -> 56.4 us
    pallas_call x1, Pallas kernels: 55.8 us -> 54.3 us  [body(): pl.pallas_call(functools.partial(kernel, img_n, txt_n), out_shape=(jax.Sh...]
where the time goes in v3:
time: 57.1 us; the launch traced here: 57 us
  Pallas kernels  56.4 us (99%)
  between operations  0.64 us (1%)
    pallas_call x1, Pallas kernels, body(): pl.pallas_call(functools.partial(kernel, img_n, txt_n), out_shape=(jax.Sh...  54.3 us
    pallas_call x1, Pallas kernels, body(): pl.pallas_call(hand_over, out_shape=(jax.ShapeDtypeStruct((1, 1), F32), j...  2.03 us

profile of v3, /device:TPU:0, one launch (start us, length us, event | category | flops | bytes accessed | tf_op | source)
XLA Modules:
  0.0 57.0 jit_solution(9698241641140464591)
XLA Ops:
  0.6 54.3 %shard_map.67 = (f32[8,128]{1,0:T(8,128)}, f32[256,512]{1,0:T(8,128)}, f32[128,512]{1,0:T(8,128)}) custom-call(bf16[1024,1280]{1,0:T(8,128)(2,1)} %timg_hbm.1, bf16[1024,1280]{1,0:T(8,128)(2,1)} %ttxt_hbm.1, bf16[1024,512]{1,0:T(8,128)(2,1)} %simg_hbm.1, bf16[1024,512]{1,0:T(8,128)(2,1)} %stxt_hbm.1), custom_call_target="tpu_custom_call" | custom-call | tf_op jit(solution)/shard_map/pallas_call | solution.py:418
  55.0 2.0 %shard_map.68 = (f32[1,1]{1,0:T(1,128)}, f32[256,512]{1,0:T(8,128)}, f32[128,512]{1,0:T(8,128)}) custom-call(f32[8,128]{1,0:T(8,128)} %get-tuple-element.9.loss, f32[256,512]{1,0:T(8,128)} %get-tuple-element.10.gimg, f32[128,512]{1,0:T(8,128)} %get-tuple-element.11.gtxt), custom_call_target="tpu_custom_call" | custom-call | tf_op jit(solution)/shard_map/pallas_call | solution.py:452
